TPU v7x, 32 devices: a whole 2x2x4 slice. The times are simulated.
32 devices in a mesh: scen: 4 (over x, core), var: 8 (over z, y).
Axes of the slice: x: 2, y: 2, z: 4, core: 2. Of those that a mesh axis runs over, the one named last changes fastest.
Arguments:
- start_point: float32 [512, 65536], P('scen', 'var'), may hold values from -1 to 1
- multipliers: float32 [512, 65536], P('scen', 'var'), may hold values from -3 to 3
- cost: bfloat16 [512, 65536], P('scen', 'var'), may hold values from -6 to 6
- curvature: bfloat16 [512, 65536], P('scen', 'var'), may hold values from 0.5 to 2
- recourse_rhs: float32 [512, 512], P('scen'), may hold values from -12 to 12
- technology: bfloat16 [512, 65536], P(None, 'var'), may hold values from -0.0234375 to 0.0234375
- scenario_weight: float32 [512], P('scen'), may hold values from 1 to 30
- previous_mean: float32 [4, 65536], P(None, 'var'), may hold values from -1 to 1
- active: int32 [512, 512], P('scen', 'var'), may hold values 0 or 1
Outputs:
- iterate: float32 [512, 65536], P('scen', 'var')
- new_multipliers: float32 [512, 65536], P('scen', 'var')
- bundle_mean: float32 [4, 65536], P(None, 'var')
- primal_norm: float32 [], replicated
- dual_norm: float32 [], replicated
All inputs are finite; a program needn't handle non-finite values. No bound on the sum of `active` on one device may be relied on, other than what follows from the above.
Results may differ from a plain program's by a relative error of at most 0.0007.
Values sent between devices are 32-bit elements; how exact they have to be, the bound alone decides.
A program may use at most 64 MiB of HBM per device.

v0:
```python
import jax
import jax.numpy as jnp
from jax import lax
from jax.sharding import PartitionSpec as P

V = 65536
BLK = 128
STEPS = 8
highest = lax.Precision.HIGHEST
penalty = 1.0
recourse_scale = 4.0
stride = 0.2
epsilon = 1e-06


def from_partner(block, axis, bit):
    count = lax.axis_size(axis)
    route = []
    for low in range(count):
        high = low | 1 << bit
        if high != low and high < count:
            route += [(low, high), (high, low)]
    return lax.ppermute(block, axis, route)


def shards(
    start_point,
    multipliers,
    cost,
    curvature,
    recourse_rhs,
    technology,
    scenario_weight,
    previous_mean,
    active,
):
    scen_rows, var_cols = start_point.shape
    groups = previous_mean.shape[0]
    group_size = lax.axis_size("scen") // groups
    position = lax.axis_index("scen")
    my_node = position // group_size
    node_of = jnp.full((scen_rows,), my_node, jnp.int32)
    member = (node_of[:, None] == jnp.arange(groups, dtype=jnp.int32)[None, :]).astype(jnp.float32)
    bundle_mass = lax.psum(jnp.sum(member * scenario_weight[:, None], axis=0), "scen")
    anchor = jnp.dot(member, previous_mean, precision=highest, preferred_element_type=jnp.float32)
    linear = cost.astype(jnp.float32) + multipliers - penalty * anchor
    diagonal = curvature.astype(jnp.float32) + penalty
    active_mask = (active > 0)[:, :, None]
    iterate = start_point
    for sweep in range(STEPS):
        rounded = iterate.astype(jnp.bfloat16)
        partial_image = lax.dot_general(
            rounded, technology, (((1,), (1,)), ((), ())), preferred_element_type=jnp.float32
        )
        image = lax.psum(partial_image, "var")
        shortfall = (image - recourse_rhs).astype(jnp.bfloat16)
        pullback = jnp.dot(shortfall, technology, preferred_element_type=jnp.float32)
        stepped = jnp.clip(
            iterate - stride * (diagonal * iterate + linear + recourse_scale * pullback), -1.0, 1.0
        )
        blocked = jnp.where(
            active_mask, stepped.reshape(scen_rows, -1, BLK), iterate.reshape(scen_rows, -1, BLK)
        )
        iterate = blocked.reshape(scen_rows, var_cols)
    weighted = scenario_weight[:, None] * iterate
    normaliser = jnp.sum(bundle_mass) * V
    own_total = jnp.sum(weighted, axis=0, keepdims=True)
    for bit in range(group_size.bit_length() - 1):
        own_total = own_total + from_partner(own_total, "scen", bit)
    own_mass = jnp.sum(
        bundle_mass * (jnp.arange(groups, dtype=jnp.int32) == my_node).astype(jnp.float32)
    )
    mean_row = own_total / own_mass
    old_row = lax.dynamic_slice_in_dim(previous_mean, my_node, 1, 0)
    leader = (position % group_size == 0).astype(jnp.float32)
    centred = iterate - mean_row
    drift_part = leader * own_mass * jnp.sum((mean_row - old_row) ** 2)
    spread_part = jnp.sum(scenario_weight[:, None] * centred * centred)
    drift_sum, spread = lax.psum((drift_part, spread_part), ("scen", "var"))
    collected = lax.all_gather(mean_row, "scen", axis=0, tiled=True)
    bundle_mean = collected.reshape(groups, group_size, var_cols)[:, 0, :]
    primal_norm = jnp.sqrt(spread / normaliser + epsilon)
    dual_norm = penalty * jnp.sqrt(drift_sum / normaliser + epsilon)
    factor = penalty * jnp.sqrt(primal_norm / dual_norm)
    new_multipliers = multipliers + factor * centred
    return (iterate, new_multipliers, bundle_mean, primal_norm, dual_norm)


def solution(mesh):
    placed = (
        P("scen", "var"),
        P("scen", "var"),
        P("scen", "var"),
        P("scen", "var"),
        P("scen", None),
        P(None, "var"),
        P("scen"),
        P(None, "var"),
        P("scen", "var"),
    )
    return jax.shard_map(
        shards,
        mesh=mesh,
        in_specs=placed,
        out_specs=(P("scen", "var"), P("scen", "var"), P(None, "var"), P(), P()),
        check_vma=False,
    )
```

profile of v0, /device:TPU:0, one launch (start us, length us, event | category | flops | bytes accessed | tf_op | source)
XLA Modules:
  0.0 788.8 jit_solution(14389353718733308539)
XLA Ops:
  7.2 0.0 all-reduce.10.cloned.1.call-start
  7.2 8.3 %fusion.55 = f32[128,512]{1,0:T(8,128)} fusion(bf16[512,8192]{1,0:T(8,128)(2,1)} %param.14, f32[128,8192]{1,0:T(8,128)} %param.9), kind=kOutput, calls=%fused_computation.68 | convolution fusion | flops 1074790400 | bytes 12845056 | tf_op jit(solution)/shard_map/dot_general | solution.py:52
  15.5 0.0 all-reduce.10.cloned.1.call-update
  15.6 0.0 all-reduce.12.cloned.1.call-start
  15.7 0.1 copy.16
  15.8 0.0 copy-start.8
  15.8 6.9 convolution_subtract_fusion
  22.8 66.7 %all-reduce.10.cloned.1.call-done = f32[128,512]{1,0:T(8,128)} async-done(((f32[128,512]{1,0:T(8,128)}), f32[128,512]{1,0:T(8,128)}) %all-reduce.10.cloned.1.call-update) | async-done | bytes 262160 | tf_op jit(solution)/shard_map/psum | solution.py:55
  89.4 2.7 broadcast_in_dim.37
  92.2 0.0 slice-start.1
  92.2 9.2 %fusion.39 = f32[128,8192]{1,0:T(8,128)S(1)} fusion(f32[128,8192]{1,0:T(8,128)} %param.9, bf16[512,8192]{1,0:T(8,128)(2,1)} %param.14, f32[128,8192]{1,0:T(8,128)} %convolution_subtract_fusion, bf16[128,8192]{1,0:T(8,128)(2,1)S(1)} %copy-done, f32[128,512]{1,0:T(8,128)} %all-reduce.10.cloned.1.call-done, f32[128,512]{1,0:T(8,128)S(1)} %copy-done.8, ...), kind=kOutput, calls=%fused_computation.48 | convolution fusion | flops 1084358656 | bytes 24641536 | tf_op jit(solution)/shard_map/dot_general | solution.py:57
  101.4 0.0 copy-start.7
  101.4 2.0 copy-done.7
  103.4 3.6 fusion.53
  107.0 0.0 all-reduce.12.cloned.1.call-update
  107.1 0.2 all-reduce.14.cloned.1.call-start
  107.3 70.2 %all-reduce.12.cloned.1.call-done = f32[128,512]{1,0:T(8,128)} async-done(((f32[128,512]{1,0:T(8,128)}), f32[128,512]{1,0:T(8,128)}) %all-reduce.12.cloned.1.call-update) | async-done | bytes 262160 | tf_op jit(solution)/shard_map/psum | solution.py:55
  177.5 9.0 %fusion.37 = f32[128,8192]{1,0:T(8,128)S(1)} fusion(f32[128,8192]{1,0:T(8,128)} %copy-done.7, bf16[512,8192]{1,0:T(8,128)(2,1)} %param.14, f32[128,8192]{1,0:T(8,128)} %convolution_subtract_fusion, bf16[128,8192]{1,0:T(8,128)(2,1)S(1)} %copy-done, f32[128,512]{1,0:T(8,128)} %all-reduce.12.cloned.1.call-done, f32[128,512]{1,0:T(8,128)S(1)} %copy-done.8, ...), kind=kOutput, calls=%fused_computation.46 | convolution fusion | flops 1084358656 | bytes 24641536 | tf_op jit(solution)/shard_map/dot_general | solution.py:57
  186.5 0.0 copy-start.2
  186.5 2.0 copy-done.2
  188.5 7.0 fusion.51
  195.5 0.0 all-reduce.14.cloned.1.call-update
  195.6 0.0 all-reduce.16.cloned.1.call-start
  195.6 70.3 %all-reduce.14.cloned.1.call-done = f32[128,512]{1,0:T(8,128)} async-done(((f32[128,512]{1,0:T(8,128)}), f32[128,512]{1,0:T(8,128)}) %all-reduce.14.cloned.1.call-update) | async-done | bytes 262160 | tf_op jit(solution)/shard_map/psum | solution.py:55
  265.9 9.0 %fusion.35 = f32[128,8192]{1,0:T(8,128)S(1)} fusion(f32[128,8192]{1,0:T(8,128)} %copy-done.2, bf16[512,8192]{1,0:T(8,128)(2,1)} %param.14, f32[128,8192]{1,0:T(8,128)} %convolution_subtract_fusion, bf16[128,8192]{1,0:T(8,128)(2,1)S(1)} %copy-done, f32[128,512]{1,0:T(8,128)} %all-reduce.14.cloned.1.call-done, f32[128,512]{1,0:T(8,128)S(1)} %copy-done.8, ...), kind=kOutput, calls=%fused_computation.44 | convolution fusion | flops 1084358656 | bytes 24641536 | tf_op jit(solution)/shard_map/dot_general | solution.py:57
  275.0 2.0 copy-done.3
  277.0 7.0 fusion.49
  284.0 0.0 all-reduce.16.cloned.1.call-update
  284.0 0.3 all-reduce.18.cloned.1.call-start
  284.3 70.1 %all-reduce.16.cloned.1.call-done = f32[128,512]{1,0:T(8,128)} async-done(((f32[128,512]{1,0:T(8,128)}), f32[128,512]{1,0:T(8,128)}) %all-reduce.16.cloned.1.call-update) | async-done | bytes 262160 | tf_op jit(solution)/shard_map/psum | solution.py:55
  354.4 9.0 %fusion.33 = f32[128,8192]{1,0:T(8,128)S(1)} fusion(f32[128,8192]{1,0:T(8,128)} %copy-done.3, bf16[512,8192]{1,0:T(8,128)(2,1)} %param.14, f32[128,8192]{1,0:T(8,128)} %convolution_subtract_fusion, bf16[128,8192]{1,0:T(8,128)(2,1)S(1)} %copy-done, f32[128,512]{1,0:T(8,128)} %all-reduce.16.cloned.1.call-done, f32[128,512]{1,0:T(8,128)S(1)} %copy-done.8, ...), kind=kOutput, calls=%fused_computation.42 | convolution fusion | flops 1084358656 | bytes 24641536 | tf_op jit(solution)/shard_map/dot_general | solution.py:57
  363.4 2.0 copy-done.4
  365.4 7.0 fusion.47
  372.4 0.0 all-reduce.18.cloned.1.call-update
  372.5 0.0 all-reduce.20.cloned.1.call-start
  372.5 70.4 %all-reduce.18.cloned.1.call-done = f32[128,512]{1,0:T(8,128)} async-done(((f32[128,512]{1,0:T(8,128)}), f32[128,512]{1,0:T(8,128)}) %all-reduce.18.cloned.1.call-update) | async-done | bytes 262160 | tf_op jit(solution)/shard_map/psum | solution.py:55
  442.9 9.0 %fusion.31 = f32[128,8192]{1,0:T(8,128)S(1)} fusion(f32[128,8192]{1,0:T(8,128)} %copy-done.4, bf16[512,8192]{1,0:T(8,128)(2,1)} %param.14, f32[128,8192]{1,0:T(8,128)} %convolution_subtract_fusion, bf16[128,8192]{1,0:T(8,128)(2,1)S(1)} %copy-done, f32[128,512]{1,0:T(8,128)} %all-reduce.18.cloned.1.call-done, f32[128,512]{1,0:T(8,128)S(1)} %copy-done.8, ...), kind=kOutput, calls=%fused_computation.40 | convolution fusion | flops 1084358656 | bytes 24641536 | tf_op jit(solution)/shard_map/dot_general | solution.py:57
  451.9 2.0 copy-done.5
  453.9 7.0 fusion.45
  460.9 0.0 all-reduce.20.cloned.1.call-update
  461.0 0.4 all-reduce.22.cloned.1.call-start
  461.4 69.9 %all-reduce.20.cloned.1.call-done = f32[128,512]{1,0:T(8,128)} async-done(((f32[128,512]{1,0:T(8,128)}), f32[128,512]{1,0:T(8,128)}) %all-reduce.20.cloned.1.call-update) | async-done | bytes 262160 | tf_op jit(solution)/shard_map/psum | solution.py:55
  531.4 9.0 %fusion.29 = f32[128,8192]{1,0:T(8,128)S(1)} fusion(f32[128,8192]{1,0:T(8,128)} %copy-done.5, bf16[512,8192]{1,0:T(8,128)(2,1)} %param.14, f32[128,8192]{1,0:T(8,128)} %convolution_subtract_fusion, bf16[128,8192]{1,0:T(8,128)(2,1)S(1)} %copy-done, f32[128,512]{1,0:T(8,128)} %all-reduce.20.cloned.1.call-done, f32[128,512]{1,0:T(8,128)S(1)} %copy-done.8, ...), kind=kOutput, calls=%fused_computation.38 | convolution fusion | flops 1084358656 | bytes 24641536 | tf_op jit(solution)/shard_map/dot_general | solution.py:57
  540.4 2.0 copy-done.6
  542.4 7.0 fusion.43
  549.4 0.0 all-reduce.22.cloned.1.call-update
  549.4 0.0 all-reduce.24.cloned.1.call-start
  549.5 70.3 %all-reduce.22.cloned.1.call-done = f32[128,512]{1,0:T(8,128)} async-done(((f32[128,512]{1,0:T(8,128)}), f32[128,512]{1,0:T(8,128)}) %all-reduce.22.cloned.1.call-update) | async-done | bytes 262160 | tf_op jit(solution)/shard_map/psum | solution.py:55
  619.8 9.0 %fusion.27 = f32[128,8192]{1,0:T(8,128)S(1)} fusion(f32[128,8192]{1,0:T(8,128)} %copy-done.6, bf16[512,8192]{1,0:T(8,128)(2,1)} %param.14, f32[128,8192]{1,0:T(8,128)} %convolution_subtract_fusion, bf16[128,8192]{1,0:T(8,128)(2,1)S(1)} %copy-done, f32[128,512]{1,0:T(8,128)} %all-reduce.22.cloned.1.call-done, f32[128,512]{1,0:T(8,128)S(1)} %copy-done.8, ...), kind=kOutput, calls=%fused_computation.36 | convolution fusion | flops 1084358656 | bytes 24641536 | tf_op jit(solution)/shard_map/dot_general | solution.py:57
  628.8 2.0 copy-done.1
  630.8 7.0 fusion.41
  637.9 0.0 all-reduce.24.cloned.1.call-update
  637.9 0.2 multiply_reduce_fusion.2
  638.1 5.8 psum.85
  643.9 0.6 fusion.60
  645.2 63.1 %all-reduce.24.cloned.1.call-done = f32[128,512]{1,0:T(8,128)} async-done(((f32[128,512]{1,0:T(8,128)}), f32[128,512]{1,0:T(8,128)}) %all-reduce.24.cloned.1.call-update) | async-done | bytes 262160 | tf_op jit(solution)/shard_map/psum | solution.py:55
  708.3 11.2 %multiply_reduce_fusion = (f32[8192]{0:T(1024)S(1)}, f32[128,8192]{1,0:T(8,128)}) fusion(f32[128]{0:T(128)S(1)} %copy-done.11, f32[128,8192]{1,0:T(8,128)} %copy-done.1, bf16[512,8192]{1,0:T(8,128)(2,1)} %param.14, f32[128,512]{1,0:T(8,128)} %all-reduce.24.cloned.1.call-done, f32[128,512]{1,0:T(8,128)S(1)} %copy-done.8, ...), kind=kOutput, calls=%fused_computation.52 | convolution fusion | flops 1086447616 | bytes 24674816 | tf_op jit(solution)/shard_map/dot_general | solution.py:57
  719.5 0.7 broadcast_divide_fusion
  720.2 0.7 multiply_reduce_fusion.1
  722.1 3.9 fusion.40
  726.1 5.4 all-gather
  731.5 39.7 %all-reduce = (f32[]{:T(128)}, f32[]{:T(128)}) all-reduce(f32[]{:T(128)} %fusion.40, f32[]{:T(128)S(6)} %mul.145), channel_id=1, replica_groups=mesh['scen'=4,'var'=8] {'scen','var'}, use_global_device_ids=true, to_apply=%region_13.14 | all-reduce | flops 2 | bytes 16 | tf_op jit(solution)/shard_map/psum | solution.py:79
  772.7 6.1 multiply_add_fusion
  778.8 0.7 reshape.75
  (21 shorter events, 0.1 us)
Async XLA Ops:
  7.2 8.5 %copy-start.10 = (s32[128,64]{0,1:T(8,128)S(1)}, s32[128,64]{0,1:T(8,128)}, u32[]{:S(2)}) copy-start(s32[128,64]{0,1:T(8,128)} %param.17) | copy-start | bytes 98308
  7.2 8.6 %copy-start.9 = (f32[4,8192]{1,0:T(4,128)S(1)}, f32[4,8192]{1,0:T(4,128)}, u32[]{:S(2)}) copy-start(f32[4,8192]{1,0:T(4,128)} %param.16) | copy-start | bytes 393220
  7.2 82.3 %all-reduce.10.cloned.1.call-start = ((), (), s32[]{:S(2)}) async-start(), calls=%async_computation | async-start | bytes 524288 | tf_op jit(solution)/shard_map/psum | solution.py:55
  15.6 161.9 %all-reduce.12.cloned.1.call-start = ((), (), s32[]{:S(2)}) async-start(), calls=%async_computation.1 | async-start | bytes 524288 | tf_op jit(solution)/shard_map/psum | solution.py:55
  15.8 76.4 %copy-start = (bf16[128,8192]{1,0:T(8,128)(2,1)S(1)}, bf16[128,8192]{1,0:T(8,128)(2,1)}, u32[]{:S(2)}) copy-start(bf16[128,8192]{1,0:T(8,128)(2,1)} %param.12) | copy-start | bytes 6291460
  15.8 76.4 %copy-start.8 = (f32[128,512]{1,0:T(8,128)S(1)}, f32[128,512]{1,0:T(8,128)}, u32[]{:S(2)}) copy-start(f32[128,512]{1,0:T(8,128)} %param.13) | copy-start | bytes 786436
  89.4 14.0 %slice-start = ((s8[8388608]{0:T(1024)(128)(4,1)}), s8[4194304]{0:T(1024)(128)(4,1)S(1)}, s32[]{:S(2)}) async-start(s8[8388608]{0:T(1024)(128)(4,1)} %bitcast.28), calls=%async_computation.8 | async-start | bytes 8388608
  92.2 11.2 %slice-start.1 = ((s8[8388608]{0:T(1024)(128)(4,1)}), s8[4194304]{0:T(1024)(128)(4,1)S(1)}, s32[]{:S(2)}) async-start(s8[8388608]{0:T(1024)(128)(4,1)} %bitcast.28), calls=%async_computation.9 | async-start | bytes 8388608
  101.4 2.0 copy-start.7
  107.1 158.9 %all-reduce.14.cloned.1.call-start = ((), (), s32[]{:S(2)}) async-start(), calls=%async_computation.2 | async-start | bytes 524288 | tf_op jit(solution)/shard_map/psum | solution.py:55
  186.5 2.0 copy-start.2
  195.6 158.8 %all-reduce.16.cloned.1.call-start = ((), (), s32[]{:S(2)}) async-start(), calls=%async_computation.3 | async-start | bytes 524288 | tf_op jit(solution)/shard_map/psum | solution.py:55
  274.9 2.0 copy-start.3
  284.0 158.9 %all-reduce.18.cloned.1.call-start = ((), (), s32[]{:S(2)}) async-start(), calls=%async_computation.4 | async-start | bytes 524288 | tf_op jit(solution)/shard_map/psum | solution.py:55
  363.4 2.0 copy-start.4
  372.5 158.9 %all-reduce.20.cloned.1.call-start = ((), (), s32[]{:S(2)}) async-start(), calls=%async_computation.5 | async-start | bytes 524288 | tf_op jit(solution)/shard_map/psum | solution.py:55
  451.9 2.0 copy-start.5
  461.0 158.8 %all-reduce.22.cloned.1.call-start = ((), (), s32[]{:S(2)}) async-start(), calls=%async_computation.6 | async-start | bytes 524288 | tf_op jit(solution)/shard_map/psum | solution.py:55
  540.4 2.0 copy-start.6
  549.4 158.8 %all-reduce.24.cloned.1.call-start = ((), (), s32[]{:S(2)}) async-start(), calls=%async_computation.7 | async-start | bytes 524288 | tf_op jit(solution)/shard_map/psum | solution.py:55
  628.8 2.0 copy-start.1
  630.8 7.1 copy-start.11
Sparse Core Ops, SparseCore 0:
  15.7 73.7 all-reduce.9
  107.2 70.2 all-reduce.11
  195.7 70.1 all-reduce.13
  284.1 70.2 all-reduce.15
  372.6 70.2 all-reduce.17
  461.1 70.2 all-reduce.19
  549.6 70.1 all-reduce.21
  638.0 70.2 all-reduce.23
where the time goes:
time: 796 us; the launch traced here: 789 us
  waiting for transfers between devices  551 us (69%)
  matrix products  135 us (17%)
  blocking collectives  50.9 us (6%)
  between operations  20.3 us (3%)
  local copies, waits for them, and re-layouts  17.6 us (2%)
  other arithmetic  12.2 us (2%)
    psum x8, waiting for transfers between devices, shards(): image = lax.psum(partial_image, 'var')  551 us
    dot_general x8, matrix products, shards(): jnp.dot(shortfall, technology, preferred_element_type=jnp.float32)  74.5 us
    dot_general x8, matrix products, shards(): lax.dot_general(rounded, technology, (((1,), (1,)), ((), ())), preferred_...  54 us
    psum x1, blocking collectives, shards(): drift_sum, spread = lax.psum((drift_part, spread_part), ('scen', 'var'))  39.7 us
  transfers between devices with their start and end apart: 8, of which 8 were waited for; matrix products, arithmetic and copies ran while one was open for 1% of the time, Pallas kernels for 0%

commit v1 on v0

--- a/solution.py
+++ b/solution.py
@@ -11,6 +11,12 @@
 recourse_scale = 4.0
 stride = 0.2
 epsilon = 1e-06
+
+
+def gather_and_add(x, axis):
+    parts = lax.all_gather(x, axis, axis=0, tiled=False)
+    total = parts.sum(axis=0)
+    return total
 
 
 def from_partner(block, axis, bit):
@@ -52,7 +58,7 @@
         partial_image = lax.dot_general(
             rounded, technology, (((1,), (1,)), ((), ())), preferred_element_type=jnp.float32
         )
-        image = lax.psum(partial_image, "var")
+        image = gather_and_add(partial_image, "var")
         shortfall = (image - recourse_rhs).astype(jnp.bfloat16)
         pullback = jnp.dot(shortfall, technology, preferred_element_type=jnp.float32)
         stepped = jnp.clip(

time: 796 us -> 637 us (0.80)
  waiting for transfers between devices: 551 us -> 372 us
  other arithmetic: 12.2 us -> 32.5 us
    psum x8 -> x0, waiting for transfers between devices: 551 us -> none  [shards(): image = lax.psum(partial_image, 'var')]
    all_gather x0 -> x8, waiting for transfers between devices: none -> 372 us  [gather_and_add(): parts = lax.all_gather(x, axis, axis=0, tiled=False)]
    reduce_sum x0 -> x8, other arithmetic: none -> 20.3 us  [gather_and_add(): total = parts.sum(axis=0)]
where the time goes in v1:
time: 637 us; the launch traced here: 629 us
  waiting for transfers between devices  372 us (58%)
  matrix products  135 us (21%)
  blocking collectives  50.6 us (8%)
  other arithmetic  32.5 us (5%)
  between operations  20.3 us (3%)
  local copies, waits for them, and re-layouts  17.7 us (3%)
    all_gather x8, waiting for transfers between devices, gather_and_add(): parts = lax.all_gather(x, axis, axis=0, tiled=False)  372 us
    dot_general x8, matrix products, shards(): jnp.dot(shortfall, technology, preferred_element_type=jnp.float32)  74.5 us
    dot_general x8, matrix products, shards(): lax.dot_general(rounded, technology, (((1,), (1,)), ((), ())), preferred_...  54.3 us
    psum x1, blocking collectives, shards(): drift_sum, spread = lax.psum((drift_part, spread_part), ('scen', 'var'))  39.4 us
    reduce_sum x8, other arithmetic, gather_and_add(): total = parts.sum(axis=0)  20.3 us
    unnamed x30, local copies, waits for them, and re-layouts  14.1 us
  transfers between devices with their start and end apart: 8, of which 8 were waited for; matrix products, arithmetic and copies ran while one was open for 1% of the time, Pallas kernels for 0%

profile of v1, /device:TPU:0, one launch (start us, length us, event | category | flops | bytes accessed | tf_op | source)
XLA Modules:
  0.0 628.8 jit_solution(12343671361552543720)
XLA Ops:
  7.2 0.0 all-gather.18.cloned.1.call-start
  7.2 8.4 %fusion.55 = f32[128,512]{1,0:T(8,128)} fusion(bf16[512,8192]{1,0:T(8,128)(2,1)} %param.14, f32[128,8192]{1,0:T(8,128)} %param.9), kind=kOutput, calls=%fused_computation.68 | convolution fusion | flops 1074790400 | bytes 12845056 | tf_op jit(solution)/shard_map/dot_general | solution.py:58
  15.7 0.0 all-gather.18.cloned.1.call-update
  15.7 0.0 all-gather.20.cloned.1.call-start
  15.8 0.1 copy.16
  15.9 6.2 convolution_subtract_fusion
  22.1 45.6 %all-gather.18.cloned.1.call-done = f32[1024,512]{1,0:T(8,128)} async-done(((f32[128,512]{1,0:T(8,128)}), f32[1024,512]{1,0:T(8,128)}) %all-gather.18.cloned.1.call-update) | async-done | bytes 2097168 | tf_op jit(solution)/shard_map/all_gather | solution.py:17
  67.7 2.5 reduce_sum.126
  70.2 2.7 broadcast_in_dim.37
  73.0 9.2 %fusion.39 = f32[128,8192]{1,0:T(8,128)S(1)} fusion(f32[128,8192]{1,0:T(8,128)} %param.9, bf16[512,8192]{1,0:T(8,128)(2,1)} %param.14, f32[128,8192]{1,0:T(8,128)} %convolution_subtract_fusion, bf16[128,8192]{1,0:T(8,128)(2,1)S(1)} %copy-done, f32[128,512]{1,0:T(8,128)} %reduce_sum.126, f32[128,512]{1,0:T(8,128)S(1)} %copy-done.8, ...), kind=kOutput, calls=%fused_computation.48 | convolution fusion | flops 1084358656 | bytes 24641536 | tf_op jit(solution)/shard_map/dot_general | solution.py:63
  82.1 2.0 copy-done.7
  84.2 3.7 fusion.53
  87.8 0.2 all-gather.22.cloned.1.call-start
  88.1 47.6 %all-gather.20.cloned.1.call-done = f32[1024,512]{1,0:T(8,128)} async-done(((f32[128,512]{1,0:T(8,128)}), f32[1024,512]{1,0:T(8,128)}) %all-gather.20.cloned.1.call-update) | async-done | bytes 2097168 | tf_op jit(solution)/shard_map/all_gather | solution.py:17
  135.6 2.5 reduce_sum.127
  138.2 9.0 %fusion.37 = f32[128,8192]{1,0:T(8,128)S(1)} fusion(f32[128,8192]{1,0:T(8,128)} %copy-done.7, bf16[512,8192]{1,0:T(8,128)(2,1)} %param.14, f32[128,8192]{1,0:T(8,128)} %convolution_subtract_fusion, bf16[128,8192]{1,0:T(8,128)(2,1)S(1)} %copy-done, f32[128,512]{1,0:T(8,128)} %reduce_sum.127, f32[128,512]{1,0:T(8,128)S(1)} %copy-done.8, ...), kind=kOutput, calls=%fused_computation.46 | convolution fusion | flops 1084358656 | bytes 24641536 | tf_op jit(solution)/shard_map/dot_general | solution.py:63
  147.2 2.0 copy-done.2
  149.2 7.0 %fusion.51 = f32[128,512]{1,0:T(8,128)} fusion(bf16[512,8192]{1,0:T(8,128)(2,1)} %param.14, f32[128,8192]{1,0:T(8,128)S(1)} %fusion.37), kind=kOutput, calls=%fused_computation.64 | convolution fusion | flops 1074790400 | bytes 12845056 | tf_op jit(solution)/shard_map/dot_general | solution.py:58
  156.2 0.0 all-gather.22.cloned.1.call-update
  156.2 0.0 all-gather.24.cloned.1.call-start
  156.3 47.7 %all-gather.22.cloned.1.call-done = f32[1024,512]{1,0:T(8,128)} async-done(((f32[128,512]{1,0:T(8,128)}), f32[1024,512]{1,0:T(8,128)}) %all-gather.22.cloned.1.call-update) | async-done | bytes 2097168 | tf_op jit(solution)/shard_map/all_gather | solution.py:17
  204.0 2.5 reduce_sum.128
  206.6 9.0 %fusion.35 = f32[128,8192]{1,0:T(8,128)S(1)} fusion(f32[128,8192]{1,0:T(8,128)} %copy-done.2, bf16[512,8192]{1,0:T(8,128)(2,1)} %param.14, f32[128,8192]{1,0:T(8,128)} %convolution_subtract_fusion, bf16[128,8192]{1,0:T(8,128)(2,1)S(1)} %copy-done, f32[128,512]{1,0:T(8,128)} %reduce_sum.128, f32[128,512]{1,0:T(8,128)S(1)} %copy-done.8, ...), kind=kOutput, calls=%fused_computation.44 | convolution fusion | flops 1084358656 | bytes 24641536 | tf_op jit(solution)/shard_map/dot_general | solution.py:63
  215.6 2.0 copy-done.3
  217.6 7.0 %fusion.49 = f32[128,512]{1,0:T(8,128)} fusion(bf16[512,8192]{1,0:T(8,128)(2,1)} %param.14, f32[128,8192]{1,0:T(8,128)S(1)} %fusion.35), kind=kOutput, calls=%fused_computation.62 | convolution fusion | flops 1074790400 | bytes 12845056 | tf_op jit(solution)/shard_map/dot_general | solution.py:58
  224.6 0.0 all-gather.24.cloned.1.call-update
  224.7 0.3 all-gather.26.cloned.1.call-start
  224.9 47.5 %all-gather.24.cloned.1.call-done = f32[1024,512]{1,0:T(8,128)} async-done(((f32[128,512]{1,0:T(8,128)}), f32[1024,512]{1,0:T(8,128)}) %all-gather.24.cloned.1.call-update) | async-done | bytes 2097168 | tf_op jit(solution)/shard_map/all_gather | solution.py:17
  272.4 2.5 reduce_sum.129
  275.0 9.0 %fusion.33 = f32[128,8192]{1,0:T(8,128)S(1)} fusion(f32[128,8192]{1,0:T(8,128)} %copy-done.3, bf16[512,8192]{1,0:T(8,128)(2,1)} %param.14, f32[128,8192]{1,0:T(8,128)} %convolution_subtract_fusion, bf16[128,8192]{1,0:T(8,128)(2,1)S(1)} %copy-done, f32[128,512]{1,0:T(8,128)} %reduce_sum.129, f32[128,512]{1,0:T(8,128)S(1)} %copy-done.8, ...), kind=kOutput, calls=%fused_computation.42 | convolution fusion | flops 1084358656 | bytes 24641536 | tf_op jit(solution)/shard_map/dot_general | solution.py:63
  284.0 2.0 copy-done.4
  286.0 7.0 %fusion.47 = f32[128,512]{1,0:T(8,128)} fusion(bf16[512,8192]{1,0:T(8,128)(2,1)} %param.14, f32[128,8192]{1,0:T(8,128)S(1)} %fusion.33), kind=kOutput, calls=%fused_computation.60 | convolution fusion | flops 1074790400 | bytes 12845056 | tf_op jit(solution)/shard_map/dot_general | solution.py:58
  293.1 0.0 all-gather.26.cloned.1.call-update
  293.1 0.0 all-gather.28.cloned.1.call-start
  293.1 47.7 %all-gather.26.cloned.1.call-done = f32[1024,512]{1,0:T(8,128)} async-done(((f32[128,512]{1,0:T(8,128)}), f32[1024,512]{1,0:T(8,128)}) %all-gather.26.cloned.1.call-update) | async-done | bytes 2097168 | tf_op jit(solution)/shard_map/all_gather | solution.py:17
  340.9 2.5 reduce_sum.130
  343.4 9.0 %fusion.31 = f32[128,8192]{1,0:T(8,128)S(1)} fusion(f32[128,8192]{1,0:T(8,128)} %copy-done.4, bf16[512,8192]{1,0:T(8,128)(2,1)} %param.14, f32[128,8192]{1,0:T(8,128)} %convolution_subtract_fusion, bf16[128,8192]{1,0:T(8,128)(2,1)S(1)} %copy-done, f32[128,512]{1,0:T(8,128)} %reduce_sum.130, f32[128,512]{1,0:T(8,128)S(1)} %copy-done.8, ...), kind=kOutput, calls=%fused_computation.40 | convolution fusion | flops 1084358656 | bytes 24641536 | tf_op jit(solution)/shard_map/dot_general | solution.py:63
  352.4 2.0 copy-done.5
  354.5 7.0 %fusion.45 = f32[128,512]{1,0:T(8,128)} fusion(bf16[512,8192]{1,0:T(8,128)(2,1)} %param.14, f32[128,8192]{1,0:T(8,128)S(1)} %fusion.31), kind=kOutput, calls=%fused_computation.58 | convolution fusion | flops 1074790400 | bytes 12845056 | tf_op jit(solution)/shard_map/dot_general | solution.py:58
  361.5 0.4 all-gather.30.cloned.1.call-start
  362.0 47.3 %all-gather.28.cloned.1.call-done = f32[1024,512]{1,0:T(8,128)} async-done(((f32[128,512]{1,0:T(8,128)}), f32[1024,512]{1,0:T(8,128)}) %all-gather.28.cloned.1.call-update) | async-done | bytes 2097168 | tf_op jit(solution)/shard_map/all_gather | solution.py:17
  409.3 2.5 reduce_sum.131
  411.8 9.0 %fusion.29 = f32[128,8192]{1,0:T(8,128)S(1)} fusion(f32[128,8192]{1,0:T(8,128)} %copy-done.5, bf16[512,8192]{1,0:T(8,128)(2,1)} %param.14, f32[128,8192]{1,0:T(8,128)} %convolution_subtract_fusion, bf16[128,8192]{1,0:T(8,128)(2,1)S(1)} %copy-done, f32[128,512]{1,0:T(8,128)} %reduce_sum.131, f32[128,512]{1,0:T(8,128)S(1)} %copy-done.8, ...), kind=kOutput, calls=%fused_computation.38 | convolution fusion | flops 1084358656 | bytes 24641536 | tf_op jit(solution)/shard_map/dot_general | solution.py:63
  420.9 2.0 copy-done.6
  422.9 7.0 %fusion.43 = f32[128,512]{1,0:T(8,128)} fusion(bf16[512,8192]{1,0:T(8,128)(2,1)} %param.14, f32[128,8192]{1,0:T(8,128)S(1)} %fusion.29), kind=kOutput, calls=%fused_computation.56 | convolution fusion | flops 1074790400 | bytes 12845056 | tf_op jit(solution)/shard_map/dot_general | solution.py:58
  429.9 0.0 all-gather.32.cloned.1.call-start
  430.0 47.7 %all-gather.30.cloned.1.call-done = f32[1024,512]{1,0:T(8,128)} async-done(((f32[128,512]{1,0:T(8,128)}), f32[1024,512]{1,0:T(8,128)}) %all-gather.30.cloned.1.call-update) | async-done | bytes 2097168 | tf_op jit(solution)/shard_map/all_gather | solution.py:17
  477.7 2.5 reduce_sum.132
  480.3 9.0 %fusion.27 = f32[128,8192]{1,0:T(8,128)S(1)} fusion(f32[128,8192]{1,0:T(8,128)} %copy-done.6, bf16[512,8192]{1,0:T(8,128)(2,1)} %param.14, f32[128,8192]{1,0:T(8,128)} %convolution_subtract_fusion, bf16[128,8192]{1,0:T(8,128)(2,1)S(1)} %copy-done, f32[128,512]{1,0:T(8,128)} %reduce_sum.132, f32[128,512]{1,0:T(8,128)S(1)} %copy-done.8, ...), kind=kOutput, calls=%fused_computation.36 | convolution fusion | flops 1084358656 | bytes 24641536 | tf_op jit(solution)/shard_map/dot_general | solution.py:63
  489.3 2.0 copy-done.1
  491.3 7.0 %fusion.41 = f32[128,512]{1,0:T(8,128)} fusion(bf16[512,8192]{1,0:T(8,128)(2,1)} %param.14, f32[128,8192]{1,0:T(8,128)S(1)} %fusion.27), kind=kOutput, calls=%fused_computation.54 | convolution fusion | flops 1074790400 | bytes 12845056 | tf_op jit(solution)/shard_map/dot_general | solution.py:58
  498.4 0.2 multiply_reduce_fusion.2
  498.6 5.8 psum.21
  504.4 0.6 fusion.60
  505.7 40.5 %all-gather.32.cloned.1.call-done = f32[1024,512]{1,0:T(8,128)} async-done(((f32[128,512]{1,0:T(8,128)}), f32[1024,512]{1,0:T(8,128)}) %all-gather.32.cloned.1.call-update) | async-done | bytes 2097168 | tf_op jit(solution)/shard_map/all_gather | solution.py:17
  546.1 2.5 reduce_sum.133
  548.7 11.2 %multiply_reduce_fusion = (f32[8192]{0:T(1024)S(1)}, f32[128,8192]{1,0:T(8,128)}) fusion(f32[128]{0:T(128)S(1)} %copy-done.12, f32[128,8192]{1,0:T(8,128)} %copy-done.1, bf16[512,8192]{1,0:T(8,128)(2,1)} %param.14, f32[128,512]{1,0:T(8,128)} %reduce_sum.133, f32[128,512]{1,0:T(8,128)S(1)} %copy-done.8, f32[128,8192]{1,0:T(8,128)} %convolution_subtract_fusion, ...), kind=kOutput, calls=%fused_computation.52 | convolution fusion | flops 1086447616 | bytes 24674816 | tf_op jit(solution)/shard_map/dot_general | solution.py:63
  559.9 0.7 broadcast_divide_fusion
  560.6 0.7 multiply_reduce_fusion.1
  562.5 3.9 fusion.40
  566.5 5.4 all-gather.8
  571.9 39.4 %all-reduce = (f32[]{:T(128)}, f32[]{:T(128)}) all-reduce(f32[]{:T(128)} %fusion.40, f32[]{:T(128)S(6)} %mul.145), channel_id=1, replica_groups=mesh['scen'=4,'var'=8] {'scen','var'}, use_global_device_ids=true, to_apply=%region_13.14 | all-reduce | flops 2 | bytes 16 | tf_op jit(solution)/shard_map/psum | solution.py:85
  612.7 6.1 multiply_add_fusion
  618.8 0.7 reshape.83
  (31 shorter events, 0.2 us)
Async XLA Ops:
  7.2 8.6 %copy-start.11 = (s32[128,64]{0,1:T(8,128)S(1)}, s32[128,64]{0,1:T(8,128)}, u32[]{:S(2)}) copy-start(s32[128,64]{0,1:T(8,128)} %param.17) | copy-start | bytes 98308
  7.2 8.7 %copy-start.9 = (bf16[128,8192]{1,0:T(8,128)(2,1)S(1)}, bf16[128,8192]{1,0:T(8,128)(2,1)}, u32[]{:S(2)}) copy-start(bf16[128,8192]{1,0:T(8,128)(2,1)} %param.11) | copy-start | bytes 6291460
  7.2 8.7 %copy-start.10 = (f32[4,8192]{1,0:T(4,128)S(1)}, f32[4,8192]{1,0:T(4,128)}, u32[]{:S(2)}) copy-start(f32[4,8192]{1,0:T(4,128)} %param.16) | copy-start | bytes 393220
  7.2 60.5 %all-gather.18.cloned.1.call-start = ((), (), s32[]{:S(2)}) async-start(), calls=%async_computation | async-start | bytes 2359296 | tf_op jit(solution)/shard_map/all_gather | solution.py:17
  15.7 119.9 %all-gather.20.cloned.1.call-start = ((), (), s32[]{:S(2)}) async-start(), calls=%async_computation.1 | async-start | bytes 2359296 | tf_op jit(solution)/shard_map/all_gather | solution.py:17
  15.9 57.0 %copy-start.8 = (f32[128,512]{1,0:T(8,128)S(1)}, f32[128,512]{1,0:T(8,128)}, u32[]{:S(2)}) copy-start(f32[128,512]{1,0:T(8,128)} %param.13) | copy-start | bytes 786436
  22.1 50.8 %copy-start = (bf16[128,8192]{1,0:T(8,128)(2,1)S(1)}, bf16[128,8192]{1,0:T(8,128)(2,1)}, u32[]{:S(2)}) copy-start(bf16[128,8192]{1,0:T(8,128)(2,1)} %param.12) | copy-start | bytes 6291460
  70.2 14.0 %slice-start = ((s8[8388608]{0:T(1024)(128)(4,1)}), s8[4194304]{0:T(1024)(128)(4,1)S(1)}, s32[]{:S(2)}) async-start(s8[8388608]{0:T(1024)(128)(4,1)} %bitcast.36), calls=%async_computation.8 | async-start | bytes 8388608
  72.9 11.2 %slice-start.1 = ((s8[8388608]{0:T(1024)(128)(4,1)}), s8[4194304]{0:T(1024)(128)(4,1)S(1)}, s32[]{:S(2)}) async-start(s8[8388608]{0:T(1024)(128)(4,1)} %bitcast.36), calls=%async_computation.9 | async-start | bytes 8388608
  82.1 2.0 copy-start.7
  87.8 116.2 %all-gather.22.cloned.1.call-start = ((), (), s32[]{:S(2)}) async-start(), calls=%async_computation.2 | async-start | bytes 2359296 | tf_op jit(solution)/shard_map/all_gather | solution.py:17
  147.2 2.0 copy-start.2
  156.2 116.2 %all-gather.24.cloned.1.call-start = ((), (), s32[]{:S(2)}) async-start(), calls=%async_computation.3 | async-start | bytes 2359296 | tf_op jit(solution)/shard_map/all_gather | solution.py:17
  215.6 2.0 copy-start.3
  224.7 116.2 %all-gather.26.cloned.1.call-start = ((), (), s32[]{:S(2)}) async-start(), calls=%async_computation.4 | async-start | bytes 2359296 | tf_op jit(solution)/shard_map/all_gather | solution.py:17
  284.0 2.0 copy-start.4
  293.1 116.2 %all-gather.28.cloned.1.call-start = ((), (), s32[]{:S(2)}) async-start(), calls=%async_computation.5 | async-start | bytes 2359296 | tf_op jit(solution)/shard_map/all_gather | solution.py:17
  352.4 2.0 copy-start.5
  361.5 116.2 %all-gather.30.cloned.1.call-start = ((), (), s32[]{:S(2)}) async-start(), calls=%async_computation.6 | async-start | bytes 2359296 | tf_op jit(solution)/shard_map/all_gather | solution.py:17
  420.9 2.0 copy-start.6
  429.9 116.2 %all-gather.32.cloned.1.call-start = ((), (), s32[]{:S(2)}) async-start(), calls=%async_computation.7 | async-start | bytes 2359296 | tf_op jit(solution)/shard_map/all_gather | solution.py:17
  489.3 2.0 copy-start.1
  491.3 7.1 %copy-start.12 = (f32[128]{0:T(128)S(1)}, f32[128]{0:T(128)}, u32[]{:S(2)}) copy-start(f32[128]{0:T(128)} %param.15) | copy-start | bytes 1540
Sparse Core Ops, SparseCore 0:
  15.8 51.8 all-gather.17
  88.0 47.6 all-gather.19
  156.4 47.6 all-gather.21
  224.8 47.6 all-gather.23
  293.2 47.6 all-gather.25
  361.6 47.6 all-gather.27
  430.1 47.6 all-gather.29
  498.5 47.6 all-gather.31
